TPU v7x, 256 devices: a whole 4x4x8 slice. The times are simulated.
256 devices in a mesh: row: 32 (over z, y), col: 8 (over x, core).
Axes of the slice: x: 4, y: 4, z: 8, core: 2. Of those that a mesh axis runs over, the one named last changes fastest.
Arguments:
- features: bfloat16 [32768, 512], P(('col', 'row')), may hold values from -6 to 6
- weight: bfloat16 [512, 512], replicated, may hold values from -0.25 to 0.25
- cotangent: bfloat16 [32768, 512], P(('row', 'col')), may hold values from -6 to 6
- blocks: bfloat16 [32, 8, 128, 128, 128], P('row', 'col'), may hold values from -6 to 6
- block_scales: float32 [32, 8, 128], P('row', 'col'), as said below
- block_rows: int32 [32, 8, 128], P('row', 'col'), may hold values from 0 to 7, as said below
- block_cols: int32 [32, 8, 128], P('row', 'col'), may hold values from 0 to 31, as said below
- block_counts: int32 [32, 8], P('row', 'col'), may hold values from 1 to 128, as said below
Outputs:
- activated: bfloat16 [32768, 512], P(('row', 'col'))
- input_grad: bfloat16 [32768, 512], P(('col', 'row'))
- weight_grad: float32 [512, 512], P(('row', 'col'))
Inputs may be any that keep to these rules, and one draw needn't show every extreme that they name: `block_rows`: within one grid cell the 128 slots name distinct block positions. `block_cols`: within one grid cell the 128 slots name distinct block positions. `block_counts`: in every draw some grid cell has all 128 slots live. `block_scales`: Positive.
All inputs are finite; a program needn't handle non-finite values.
Results may differ from a plain program's by a relative error of at most 0.0063.
Values may be sent and summed in bfloat16 or wider, within the bound.
No kernel may reach another device: no remote copies, remote signals or barrier semaphores. Data moves between devices by JAX's collectives and lax.ppermute only.
A program may use at most 64 MiB of HBM per device.

v0:
```python
import math

import jax
import jax.numpy as jnp
from jax import lax
from jax.sharding import PartitionSpec as P


def silu_slope(values):
    sigmoid_part = jax.nn.sigmoid(values)
    return sigmoid_part * (1.0 + values * (1.0 - sigmoid_part))


def group_loop(stop_pos, position_cap, step_fn, carry):
    group_len = min(16, position_cap)
    last_group = (jnp.asarray(stop_pos, jnp.int32) + group_len - 1) // group_len

    def one_group(group_idx, state):
        places = group_idx * group_len + jnp.arange(group_len, dtype=jnp.int32)
        live_mask = (places < stop_pos).astype(jnp.float32)
        places = jnp.minimum(places, position_cap - 1)
        return step_fn(state, places, live_mask)

    return lax.fori_loop(jnp.int32(0), last_group, one_group, carry)


def shards(features, weight, cotangent, blocks, block_scales, block_rows, block_cols, block_counts):
    row_devices = lax.axis_size("row")
    col_devices = lax.axis_size("col")
    adj_tiles = blocks[0, 0]
    own_scales = block_scales[0, 0]
    own_rows = block_rows[0, 0]
    own_cols = block_cols[0, 0]
    own_count = block_counts[0, 0]
    node_rows, feature_width = features.shape
    slot_total = adj_tiles.shape[0]
    block_size = adj_tiles.shape[2]
    tile_rows = node_rows * col_devices
    tile_cols = node_rows * row_devices
    row_blocks = tile_rows // block_size
    col_blocks = tile_cols // block_size
    projected = jnp.dot(features, weight, preferred_element_type=jnp.float32).astype(jnp.bfloat16)
    gathered = lax.all_gather(projected, "row", axis=0, tiled=True)
    feat_blocks = gathered.reshape(col_blocks, block_size, feature_width)

    def forward_add(state, places, live_mask):
        chosen_tiles = jnp.take(adj_tiles, places, axis=0)
        chosen_feats = jnp.take(feat_blocks, jnp.take(own_cols, places), axis=0)
        products = jnp.einsum(
            "gij,gjf->gif", chosen_tiles, chosen_feats, preferred_element_type=jnp.float32
        )
        factor = jnp.take(own_scales, places) * live_mask
        return state.at[jnp.take(own_rows, places)].add(products * factor[:, None, None])

    forward_init = jnp.zeros((row_blocks, block_size, feature_width), jnp.float32)
    partial_value = group_loop(own_count, slot_total, forward_add, forward_init).reshape(
        tile_rows, feature_width
    )
    mine = lax.psum_scatter(partial_value, "col", scatter_dimension=0, tiled=True)
    activated = jax.nn.silu(mine).astype(jnp.bfloat16)
    grad_share = (cotangent.astype(jnp.float32) * silu_slope(mine)).astype(jnp.bfloat16)
    grad_tile = lax.all_gather(grad_share, "col", axis=0, tiled=True)
    grad_blocks = grad_tile.reshape(row_blocks, block_size, feature_width)

    def backward_add(state, places, live_mask):
        chosen_tiles = jnp.take(adj_tiles, places, axis=0)
        chosen_grads = jnp.take(grad_blocks, jnp.take(own_rows, places), axis=0)
        products = jnp.einsum(
            "gji,gjf->gif", chosen_tiles, chosen_grads, preferred_element_type=jnp.float32
        )
        factor = jnp.take(own_scales, places) * live_mask
        return state.at[jnp.take(own_cols, places)].add(products * factor[:, None, None])

    backward_init = jnp.zeros((col_blocks, block_size, feature_width), jnp.float32)
    backward_tiles = group_loop(own_count, slot_total, backward_add, backward_init).reshape(
        tile_cols, feature_width
    )
    back_share = lax.psum_scatter(backward_tiles, "row", scatter_dimension=0, tiled=True)
    proj_grad = back_share.astype(jnp.bfloat16)
    input_grad = lax.dot_general(
        proj_grad, weight, (((1,), (1,)), ((), ())), preferred_element_type=jnp.float32
    ).astype(jnp.bfloat16)
    node_total = node_rows * row_devices * col_devices
    local_grad = lax.dot_general(
        features, proj_grad, (((0,), (0,)), ((), ())), preferred_element_type=jnp.float32
    )
    weight_grad = lax.psum_scatter(local_grad, ("row", "col"), scatter_dimension=0, tiled=True) * (
        1.0 / math.sqrt(node_total)
    )
    return (activated, input_grad, weight_grad)


def solution(mesh):
    return jax.shard_map(
        shards,
        mesh=mesh,
        in_specs=(
            P(("col", "row"), None),
            P(),
            P(("row", "col"), None),
            P("row", "col", None, None, None),
            P("row", "col", None),
            P("row", "col", None),
            P("row", "col", None),
            P("row", "col"),
        ),
        out_specs=(P(("row", "col"), None), P(("col", "row"), None), P(("row", "col"), None)),
        check_vma=False,
    )
```

profile of v0, /device:TPU:2, one launch (start us, length us, event | category | flops | bytes accessed | tf_op | source)
XLA Modules:
  0.0 999.7 jit_solution(18130673358289178238)
XLA Ops:
  10.7 85.2 %all-gather.3.cloned.1.call-done = bf16[4096,512]{1,0:T(8,128)(2,1)} async-done(((bf16[128,512]{1,0:T(8,128)(2,1)}), bf16[4096,512]{1,0:T(8,128)(2,1)}) %all-gather.3.cloned.1.call-update) | async-done | bytes 4194320 | tf_op jit(solution)/shard_map/all_gather | solution.py:43
  96.2 66.9 %while.20 = (s32[]{:T(128)}, f32[8,128,512]{2,1,0:T(8,128)S(1)}, s32[]{:T(128)}, s32[128]{0:T(128)}, bf16[128,128,128]{2,1,0:T(8,128)(2,1)}, /*index=5*/s32[128]...) while((s32[]{:T(128)}, f32[8,128,512]{2,1,0:T(8,128)S(1)}, ...), condition=%wide.region_2.0_spmd, body=%wide.region_0.5_spmd.sunk | while | flops 271846080 | bytes 24651348 | solution.py:24
  101.0 4.2 gather_fusion.3
  108.0 4.3 convolution_multiply_fusion.4
  112.4 6.2 scatter_fusion
  123.3 4.2 gather_fusion.3
  130.3 4.3 convolution_multiply_fusion.4
  134.7 6.2 scatter_fusion
  145.5 4.2 gather_fusion.3
  152.6 4.3 convolution_multiply_fusion.4
  156.9 6.1 scatter_fusion
  164.5 140.5 %reduce-scatter.4.cloned.1.call-done = f32[128,512]{1,0:T(8,128)} async-done(((f32[1024,512]{1,0:T(8,128)}), f32[128,512]{1,0:T(8,128)}) %reduce-scatter.4.cloned.1.call-update) | async-done | bytes 262160 | tf_op jit(solution)/shard_map/reduce_scatter | solution.py:59
  306.8 26.9 %all-gather.5.cloned.1.call-done = bf16[1024,512]{1,0:T(8,128)(2,1)} async-done(((bf16[128,512]{1,0:T(8,128)(2,1)}), bf16[1024,512]{1,0:T(8,128)(2,1)}) %all-gather.5.cloned.1.call-update) | async-done | bytes 1048592 | tf_op jit(solution)/shard_map/all_gather | solution.py:62
  333.7 4.3 broadcast_in_dim.54
  338.0 60.3 %while.21 = (s32[]{:T(128)}, f32[32,128,512]{2,1,0:T(8,128)}, s32[]{:T(128)}, s32[128]{0:T(128)S(1)}, bf16[128,128,128]{2,1,0:T(8,128)(2,1)}, /*index=5*/s32[128...) while((s32[]{:T(128)}, f32[32,128,512]{2,1,0:T(8,128)}, ...), condition=%wide.region_6.10_spmd, body=%wide.region_4.9_spmd.sunk | while | flops 271846080 | bytes 24651348 | solution.py:24
  342.6 2.8 gather_fusion.9
  345.5 3.0 convolution_multiply_fusion.5
  348.5 9.7 scatter_fusion.1
  365.6 3.0 convolution_multiply_fusion.5
  368.6 9.6 scatter_fusion.1
  385.6 3.0 convolution_multiply_fusion.5
  388.6 9.6 scatter_fusion.1
  398.3 330.5 %reduce-scatter.6.cloned.1.call-done = f32[128,512]{1,0:T(8,128)} async-done(((f32[4096,512]{1,0:T(8,128)}), f32[128,512]{1,0:T(8,128)}) %reduce-scatter.6.cloned.1.call-update) | async-done | bytes 262160 | tf_op jit(solution)/shard_map/reduce_scatter | solution.py:78
  733.0 258.4 %all-reduce.3.cloned.1.call-done = f32[512,512]{0,1:T(8,128)} async-done(((f32[512,512]{0,1:T(8,128)}), f32[512,512]{0,1:T(8,128)}) %all-reduce.3.cloned.1.call-update) | async-done | bytes 1048592
  (93 shorter events, 54.4 us)
Async XLA Ops:
  7.2 1.0 copy-start
  7.2 88.8 %all-gather.3.cloned.1.call-start = ((), (), s32[]{:S(2)}) async-start(), calls=%async_computation.2 | async-start | bytes 4325376 | tf_op jit(solution)/shard_map/all_gather | solution.py:43
  10.0 295.0 %reduce-scatter.4.cloned.1.call-start = ((), (), s32[]{:S(2)}) async-start(), calls=%async_computation.3 | async-start | bytes 2359296 | tf_op jit(solution)/shard_map/reduce_scatter | solution.py:59
  96.2 208.8 %copy-start.6 = (bf16[128,512]{1,0:T(8,128)(2,1)S(1)}, bf16[128,512]{1,0:T(8,128)(2,1)}, u32[]{:S(2)}) copy-start(bf16[128,512]{1,0:T(8,128)(2,1)} %param.20) | copy-start | bytes 393220
  163.1 1.3 copy-start.4
  164.4 169.2 %all-gather.5.cloned.1.call-start = ((), (), s32[]{:S(2)}) async-start(), calls=%async_computation.4 | async-start | bytes 1179648 | tf_op jit(solution)/shard_map/all_gather | solution.py:62
  306.8 422.0 %reduce-scatter.6.cloned.1.call-start = ((), (), s32[]{:S(2)}) async-start(), calls=%async_computation.5 | async-start | bytes 8650752 | tf_op jit(solution)/shard_map/reduce_scatter | solution.py:78
  333.7 4.3 copy-start.1
  333.7 4.3 copy-start.2
  333.7 4.3 copy-start.3
  398.2 330.6 %copy-start.5 = (bf16[128,512]{1,0:T(8,128)(2,1)S(1)}, bf16[128,512]{1,0:T(8,128)(2,1)}, u32[]{:S(2)}) copy-start(bf16[128,512]{1,0:T(8,128)(2,1)} %param.18) | copy-start | bytes 393220
  398.3 593.1 %all-reduce.3.cloned.1.call-start = ((), (), s32[]{:S(2)}) async-start(), calls=%async_computation.6 | async-start | bytes 2097152
Sparse Core Ops, SparseCore 0:
  11.1 84.7 all-gather.2
  164.6 140.3 reduce-scatter.3
  307.4 26.2 all-gather.4
  398.4 330.3 reduce-scatter.5
  734.1 257.2 all-reduce.2
where the time goes:
time: 1000 us
  waiting for transfers between devices  841 us (84%)
  local copies, waits for them, and re-layouts  60.8 us (6%)
  other arithmetic  54.4 us (5%)
  matrix products  27.9 us (3%)
  between operations  14.5 us (1%)
    reduce_scatter x1, waiting for transfers between devices, shards(): lax.psum_scatter(backward_tiles, 'row', scatter_dimension=0, tiled=True)  330 us
    unnamed x6, waiting for transfers between devices  258 us
    reduce_scatter x1, waiting for transfers between devices, shards(): lax.psum_scatter(partial_value, 'col', scatter_dimension=0, tiled=True)  140 us
    all_gather x1, waiting for transfers between devices, shards(): gathered = lax.all_gather(projected, 'row', axis=0, tiled=True)  85.2 us
    scatter-add x3, other arithmetic, backward_add(): state.at[jnp.take(own_cols, places)].add(products * factor[:, None, None])  28.9 us
    all_gather x1, waiting for transfers between devices, shards(): grad_tile = lax.all_gather(grad_share, 'col', axis=0, tiled=True)  26.9 us
  transfers between devices with their start and end apart: 5, of which 5 were waited for; matrix products, arithmetic and copies ran while one was open for 0% of the time, Pallas kernels for 0%

commit v1 on v0

v1 whole, which is shorter than its diff:
```python
import math

import jax
import jax.numpy as jnp
import numpy as np
from jax import lax
from jax.experimental import pallas as pl
from jax.experimental.pallas import tpu as pltpu
from jax.sharding import Mesh
from jax.sharding import PartitionSpec as P

BF = jnp.bfloat16
F32 = jnp.float32
NZ, NY, NX, NC = 8, 4, 4, 2
ROW = ("z", "y")
COL = ("x", "c")
BLK = 128
BROWS = NX * NC
BCOLS = NZ * NY
FEAT = 512


def build_kernel(cnt, rows, cols, scl, blk, dense, dense_t):
    dense[...] = jnp.zeros_like(dense)
    dense_t[...] = jnp.zeros_like(dense_t)

    def one(s, carry):
        r, c = rows[s], cols[s]
        tile = blk[s].astype(F32) * scl[s]
        ct = (c % NY) * NZ + c // NY
        r0 = pl.multiple_of(r * BLK, BLK)
        c0 = pl.multiple_of(c * BLK, BLK)
        t0 = pl.multiple_of(ct * BLK, BLK)
        dense[pl.ds(r0, BLK), pl.ds(c0, BLK)] = tile.astype(BF)
        dense_t[pl.ds(t0, BLK), pl.ds(r0, BLK)] = tile.T.astype(BF)
        return carry

    lax.fori_loop(0, cnt[0], one, 0)


def build(cnt, rows, cols, scl, blk):
    smem = pl.BlockSpec(memory_space=pltpu.SMEM)
    vmem = pl.BlockSpec(memory_space=pltpu.VMEM)
    return pl.pallas_call(
        build_kernel,
        out_shape=(
            jax.ShapeDtypeStruct((BROWS * BLK, BCOLS * BLK), BF),
            jax.ShapeDtypeStruct((BCOLS * BLK, BROWS * BLK), BF),
        ),
        in_specs=[smem, smem, smem, smem, vmem],
        out_specs=(vmem, vmem),
        compiler_params=pltpu.CompilerParams(vmem_limit_bytes=40 << 20),
        cost_estimate=pl.CostEstimate(flops=1 << 22, bytes_accessed=20 << 20, transcendentals=0),
    )(cnt, rows, cols, scl, blk)


def shards(features, weight, cotangent, blocks, block_scales, block_rows, block_cols, block_counts):
    cnt = block_counts.reshape(1)
    dense, dense_t = build(
        cnt, block_rows.reshape(-1), block_cols.reshape(-1), block_scales.reshape(-1), blocks[0, 0]
    )
    feat_y = lax.all_gather(features, "y", axis=0, tiled=True)
    feat = lax.all_gather(feat_y, "z", axis=0, tiled=True)
    part = jnp.dot(dense, feat, preferred_element_type=F32).astype(BF)
    part = lax.all_to_all(part.reshape(BROWS, BLK, FEAT), COL, 0, 0)
    hid = jnp.sum(part.astype(F32), axis=0).astype(BF)
    agg = jnp.dot(hid, weight, preferred_element_type=F32)
    sig = jax.nn.sigmoid(agg)
    activated = (agg * sig).astype(BF)
    pre = (cotangent.astype(F32) * (sig * (1.0 + agg * (1.0 - sig)))).astype(BF)
    wpart = lax.dot_general(hid, pre, (((0,), (0,)), ((), ())), preferred_element_type=F32).astype(BF)
    grad = lax.dot_general(pre, weight, (((1,), (1,)), ((), ())), preferred_element_type=F32).astype(BF)
    grad = lax.all_gather(grad, COL, axis=0, tiled=True)
    wall = lax.all_to_all(wpart.reshape(NZ * NY * NX * NC, 2, FEAT), ROW + COL, 0, 0)
    nodes = BLK * NZ * NY * NX * NC
    weight_grad = jnp.sum(wall.astype(F32), axis=0) * (1.0 / math.sqrt(nodes))
    back = jnp.dot(dense_t, grad, preferred_element_type=F32).astype(BF)
    back = lax.all_to_all(back.reshape(NY, NZ * BLK, FEAT), "y", 0, 0)
    back = jnp.sum(back.astype(F32), axis=0).astype(BF)
    back = lax.all_to_all(back.reshape(NZ, BLK, FEAT), "z", 0, 0)
    input_grad = jnp.sum(back.astype(F32), axis=0).astype(BF)
    return (activated, input_grad, weight_grad)


def solution(mesh):
    mesh4 = Mesh(np.asarray(mesh.devices).reshape(NZ, NY, NX, NC), ("z", "y", "x", "c"))
    return jax.shard_map(
        shards,
        mesh=mesh4,
        in_specs=(
            P(COL + ROW, None),
            P(),
            P(ROW + COL, None),
            P(ROW, COL, None, None, None),
            P(ROW, COL, None),
            P(ROW, COL, None),
            P(ROW, COL, None),
            P(ROW, COL),
        ),
        out_specs=(P(ROW + COL, None), P(COL + ROW, None), P(ROW + COL, None)),
        check_vma=False,
    )
```

time: 1000 us -> 269 us (0.27)
  waiting for transfers between devices: 841 us -> 156 us
  local copies, waits for them, and re-layouts: 60.8 us -> 8.41 us
  other arithmetic: 54.4 us -> 6.17 us
  blocking collectives: 0 us -> 34.4 us
  starting transfers between devices: 0.2 us -> 19.8 us
    reduce_scatter x2 -> x0, waiting for transfers between devices: 471 us -> none  [the longest x1 330 us: shards(): lax.psum_scatter(backward_tiles, 'row', scatter_dimension=0, tiled=True)]
    unnamed x6 -> x2, waiting for transfers between devices: 258 us -> 0.03 us
    all_to_all x0 -> x3, waiting for transfers between devices: none -> 91 us  [the longest x1 48.1 us: shards(): back = lax.all_to_all(back.reshape(NY, NZ * BLK, FEAT), 'y', 0, 0)]
    gather x30 -> x0, local copies, waits for them, and re-layouts: 53.2 us -> none  [the longest x6 16.7 us: forward_add(): chosen_feats = jnp.take(feat_blocks, jnp.take(own_cols, places), axis=0)]
    scatter-add x6 -> x0, other arithmetic: 47.3 us -> none  [the longest x3 28.9 us: backward_add(): state.at[jnp.take(own_cols, places)].add(products * factor[:, None, None])]
    all_gather x2, waiting for transfers between devices: 112 us -> 65.3 us  [the longest x1 43.3 us: shards(): feat = lax.all_gather(feat_y, 'z', axis=0, tiled=True)]
    all_to_all x0 -> x3, starting transfers between devices: none -> 19.8 us  [the longest x1 11.4 us: shards(): lax.all_to_all(wpart.reshape(NZ * NY * NX * NC, 2, FEAT), ROW + COL, 0, 0)]
    all_to_all x0 -> x1, blocking collectives: none -> 19.2 us  [shards(): part = lax.all_to_all(part.reshape(BROWS, BLK, FEAT), COL, 0, 0)]
  transfers between devices with their start and end apart: 5 -> 5, of which waited for: 5 -> 5; matrix products, arithmetic and copies ran while one was open for 0% -> 2% of each run, Pallas kernels for 0% -> 2%
where the time goes in v1:
time: 269 us; the launch traced here: 266 us
  waiting for transfers between devices  156 us (58%)
  blocking collectives  34.4 us (13%)
  matrix products  21.5 us (8%)
  starting transfers between devices  19.8 us (7%)
  between operations  14.8 us (6%)
  local copies, waits for them, and re-layouts  8.41 us (3%)
  other arithmetic  6.17 us (2%)
  Pallas kernels  4.96 us (2%)
    all_to_all x1, waiting for transfers between devices, shards(): back = lax.all_to_all(back.reshape(NY, NZ * BLK, FEAT), 'y', 0, 0)  48.1 us
    all_gather x1, waiting for transfers between devices, shards(): feat = lax.all_gather(feat_y, 'z', axis=0, tiled=True)  43.3 us
    all_to_all x1, waiting for transfers between devices, shards(): back = lax.all_to_all(back.reshape(NZ, BLK, FEAT), 'z', 0, 0)  27.8 us
    all_gather x1, waiting for transfers between devices, shards(): grad = lax.all_gather(grad, COL, axis=0, tiled=True)  21.9 us
    all_to_all x1, blocking collectives, shards(): part = lax.all_to_all(part.reshape(BROWS, BLK, FEAT), COL, 0, 0)  19.2 us
    all_gather x1, blocking collectives, shards(): feat_y = lax.all_gather(features, 'y', axis=0, tiled=True)  15.2 us
    all_to_all x1, waiting for transfers between devices, shards(): lax.all_to_all(wpart.reshape(NZ * NY * NX * NC, 2, FEAT), ROW + COL, 0, 0)  15.1 us
    all_to_all x1, starting transfers between devices, shards(): lax.all_to_all(wpart.reshape(NZ * NY * NX * NC, 2, FEAT), ROW + COL, 0, 0)  11.4 us
  transfers between devices with their start and end apart: 5, of which 5 were waited for; matrix products, arithmetic and copies ran while one was open for 2% of the time, Pallas kernels for 2%

profile of v1, /device:TPU:2, one launch (start us, length us, event | category | flops | bytes accessed | tf_op | source)
XLA Modules:
  0.0 266.3 jit_solution(4767257126790209541)
XLA Ops:
  7.2 15.2 %all_gather.9 = bf16[512,512]{1,0:T(8,128)(2,1)} all-gather(bf16[128,512]{1,0:T(8,128)(2,1)} %param.8), channel_id=1, replica_groups=mesh['z'=8,'y'=4,'x'=4,'c'=2] {'y'}, dimensions={0}, use_global_device_ids=true | all-gather | bytes 655360 | tf_op jit(solution)/shard_map/all_gather | solution.py:62
  23.2 2.2 copy-done.1
  25.4 0.7 copy-done.2
  26.0 0.7 copy-done.3
  26.7 0.7 copy-done.4
  27.3 5.0 %shard_map.103 = (bf16[1024,4096]{1,0:T(8,128)(2,1)S(1)}, bf16[4096,1024]{1,0:T(8,128)(2,1)}) custom-call(s32[1]{0:T(128)} %bitcast.16.cnt, s32[128]{0:T(128)S(1)} %bitcast.18, s32[128]{0:T(128)S(1)} %bitcast.19, f32[128]{0:T(128)S(1)} %bitcast.20, bf16[128,128,128]{2,1,0:T(8,128)(2,1)S(1)} %bitcast.17), custom_call_target="tpu_custom_call" | custom-call | flops 4194304 | bytes 20971520 | tf_op jit(solution)/shard_map/pallas_call | solution.py:44
  32.3 3.2 %copy-done.5 = bf16[1024,4096]{1,0:T(8,128)(2,1)} copy-done((bf16[1024,4096]{1,0:T(8,128)(2,1)}, bf16[1024,4096]{1,0:T(8,128)(2,1)S(1)}, u32[]{:S(2)}) %copy-start.5) | copy-done | bytes 8388632
  35.5 43.3 %all-gather.3.cloned.1.call-done = bf16[4096,512]{1,0:T(8,128)(2,1)} async-done(((bf16[512,512]{1,0:T(8,128)(2,1)}), bf16[4096,512]{1,0:T(8,128)(2,1)}) %all-gather.3.cloned.1.call-update) | async-done | bytes 4194320 | tf_op jit(solution)/shard_map/all_gather | solution.py:63
  78.8 9.1 %convolution_convert_fusion.1 = bf16[1024,512]{1,0:T(8,128)(2,1)S(1)} fusion(bf16[1024,4096]{1,0:T(8,128)(2,1)} %copy-done.5, bf16[4096,512]{1,0:T(8,128)(2,1)} %all-gather.3.cloned.1.call-done), kind=kOutput, calls=%fused_computation.1 | convolution fusion | flops 4295491584 | bytes 13631488 | tf_op jit(solution)/shard_map/dot_general | solution.py:64
  87.9 19.2 %all_to_all.20 = bf16[8,128,512]{2,1,0:T(8,128)(2,1)S(1)} all-to-all(bf16[8,128,512]{2,1,0:T(8,128)(2,1)S(1)} %bitcast.22), channel_id=1, replica_groups=mesh['z'=8,'y'=4,'x'=4,'c'=2] {'x','c'}, dimensions={0} | all-to-all | bytes 2097152 | tf_op jit(solution)/shard_map/all_to_all | solution.py:65
  107.3 0.9 multiply_convert_fusion.1
  108.2 1.0 convolution_convert_fusion.3
  109.2 21.9 %all-gather.5.cloned.1.call-done = bf16[1024,512]{1,0:T(8,128)(2,1)} async-done(((bf16[128,512]{1,0:T(8,128)(2,1)}), bf16[1024,512]{1,0:T(8,128)(2,1)}) %all-gather.5.cloned.1.call-update) | async-done | bytes 1048592 | tf_op jit(solution)/shard_map/all_gather | solution.py:73
  131.2 10.1 %convolution_convert_fusion = bf16[4096,512]{1,0:T(8,128)(2,1)} fusion(bf16[4096,1024]{1,0:T(8,128)(2,1)} %get-tuple-element.6, bf16[1024,512]{1,0:T(8,128)(2,1)} %all-gather.5.cloned.1.call-done), kind=kOutput, calls=%fused_computation | convolution fusion | flops 4297064448 | bytes 13631488 | tf_op jit(solution)/shard_map/dot_general | solution.py:77
  141.3 4.8 %all-to-all-start.1 = ((bf16[4,1024,512]{2,1,0:T(8,128)(2,1)}), bf16[4,1024,512]{2,1,0:T(8,128)(2,1)}, u32[]{:S(2)}, u32[]{:S(2)}) async-start(bf16[4,1024,512]{2,1,0:T(8,128)(2,1)} %bitcast.21), calls=%async_computation.1 | async-start | bytes 8388608 | tf_op jit(solution)/shard_map/all_to_all | solution.py:78
  146.5 1.0 reshape.37
  147.5 48.1 %all-to-all-done.1 = bf16[4,1024,512]{2,1,0:T(8,128)(2,1)} async-done(((bf16[4,1024,512]{2,1,0:T(8,128)(2,1)}), bf16[4,1024,512]{2,1,0:T(8,128)(2,1)}, u32[]{:S(2)}, u32[]{:S(2)}) %all-to-all-start.1) | async-done | bytes 4194336 | tf_op jit(solution)/shard_map/all_to_all | solution.py:78
  195.6 11.4 %all-to-all-start.3 = ((bf16[256,2,512]{2,1,0:T(2,128)(2,1)}), bf16[256,2,512]{2,1,0:T(2,128)(2,1)S(1)}, u32[]{:S(2)}, u32[]{:S(2)}) async-start(bf16[256,2,512]{2,1,0:T(2,128)(2,1)} %reshape.37), calls=%async_computation.3 | async-start | bytes 1048576 | tf_op jit(solution)/shard_map/all_to_all | solution.py:74
  207.0 4.1 %reduce_sum.46 = bf16[1024,512]{1,0:T(8,128)(2,1)} reduce(bf16[4,1024,512]{2,1,0:T(8,128)(2,1)} %all-to-all-done.1, bf16[]{:T(256)} %constant.6.clone.1), dimensions={0}, to_apply=%region_1.0 | reduce | flops 1572864 | bytes 5242882 | tf_op jit(solution)/shard_map/reduce_sum | solution.py:79
  211.1 15.1 %all-to-all-done.3 = bf16[256,2,512]{2,1,0:T(2,128)(2,1)S(1)} async-done(((bf16[256,2,512]{2,1,0:T(2,128)(2,1)}), bf16[256,2,512]{2,1,0:T(2,128)(2,1)S(1)}, u32[]{:S(2)}, u32[]{:S(2)}) %all-to-all-start.3) | async-done | bytes 524320 | tf_op jit(solution)/shard_map/all_to_all | solution.py:74
  226.2 3.6 %all-to-all-start.2 = ((bf16[8,128,512]{2,1,0:T(8,128)(2,1)}), bf16[8,128,512]{2,1,0:T(8,128)(2,1)S(1)}, u32[]{:S(2)}, u32[]{:S(2)}) async-start(bf16[8,128,512]{2,1,0:T(8,128)(2,1)} %bitcast.7), calls=%async_computation.2 | async-start | bytes 2097152 | tf_op jit(solution)/shard_map/all_to_all | solution.py:80
  230.3 0.6 broadcast_multiply_fusion
  230.9 27.8 %all-to-all-done.2 = bf16[8,128,512]{2,1,0:T(8,128)(2,1)S(1)} async-done(((bf16[8,128,512]{2,1,0:T(8,128)(2,1)}), bf16[8,128,512]{2,1,0:T(8,128)(2,1)S(1)}, u32[]{:S(2)}, u32[]{:S(2)}) %all-to-all-start.2) | async-done | bytes 1048608 | tf_op jit(solution)/shard_map/all_to_all | solution.py:80
  258.7 0.8 reduce_sum.47
  (16 shorter events, 1.2 us)
Async XLA Ops:
  7.2 100.1 %copy-start = (bf16[512,512]{1,0:T(8,128)(2,1)S(1)}, bf16[512,512]{1,0:T(8,128)(2,1)}, u32[]{:S(2)}) copy-start(bf16[512,512]{1,0:T(8,128)(2,1)} %param.9) | copy-start | bytes 1572868
  7.2 71.6 %all-gather.3.cloned.1.call-start = ((), (), s32[]{:S(2)}) async-start(), calls=%async_computation.4 | async-start | bytes 4718592 | tf_op jit(solution)/shard_map/all_gather | solution.py:63
  22.5 108.7 %all-gather.5.cloned.1.call-start = ((), (), s32[]{:S(2)}) async-start(), calls=%async_computation.5 | async-start | bytes 1179648 | tf_op jit(solution)/shard_map/all_gather | solution.py:73
  23.2 2.2 copy-start.1
  25.4 0.7 copy-start.2
  26.0 0.7 copy-start.3
  26.7 0.7 copy-start.4
  32.3 3.2 %copy-start.5 = (bf16[1024,4096]{1,0:T(8,128)(2,1)}, bf16[1024,4096]{1,0:T(8,128)(2,1)S(1)}, u32[]{:S(2)}) copy-start(bf16[1024,4096]{1,0:T(8,128)(2,1)S(1)} %get-tuple-element.5) | copy-start | bytes 25165828
  78.8 29.4 %copy-start.6 = (bf16[128,512]{1,0:T(8,128)(2,1)S(1)}, bf16[128,512]{1,0:T(8,128)(2,1)}, u32[]{:S(2)}) copy-start(bf16[128,512]{1,0:T(8,128)(2,1)} %param.10) | copy-start | bytes 393220
  141.3 54.4 %all-to-all-start.1 = ((bf16[4,1024,512]{2,1,0:T(8,128)(2,1)}), bf16[4,1024,512]{2,1,0:T(8,128)(2,1)}, u32[]{:S(2)}, u32[]{:S(2)}) async-start(bf16[4,1024,512]{2,1,0:T(8,128)(2,1)} %bitcast.21), calls=%async_computation.1 | async-start | bytes 8388608 | tf_op jit(solution)/shard_map/all_to_all | solution.py:78
  195.6 30.6 %all-to-all-start.3 = ((bf16[256,2,512]{2,1,0:T(2,128)(2,1)}), bf16[256,2,512]{2,1,0:T(2,128)(2,1)S(1)}, u32[]{:S(2)}, u32[]{:S(2)}) async-start(bf16[256,2,512]{2,1,0:T(2,128)(2,1)} %reshape.37), calls=%async_computation.3 | async-start | bytes 1048576 | tf_op jit(solution)/shard_map/all_to_all | solution.py:74
  226.2 32.4 %all-to-all-start.2 = ((bf16[8,128,512]{2,1,0:T(8,128)(2,1)}), bf16[8,128,512]{2,1,0:T(8,128)(2,1)S(1)}, u32[]{:S(2)}, u32[]{:S(2)}) async-start(bf16[8,128,512]{2,1,0:T(8,128)(2,1)} %bitcast.7), calls=%async_computation.2 | async-start | bytes 2097152 | tf_op jit(solution)/shard_map/all_to_all | solution.py:80
Sparse Core Ops, SparseCore 0:
  22.6 56.1 all-gather.2
  109.3 21.7 all-gather.4
